TPU v7x, 32 devices: a whole 2x2x4 slice. The times are simulated.
32 devices in a mesh: samp: 4 (over x, core), feat: 8 (over z, y).
Axes of the slice: x: 2, y: 2, z: 4, core: 2. Of those that a mesh axis runs over, the one named last changes fastest.
Arguments:
- design: float32 [4096, 65536], P('samp', 'feat'), may hold values from -0.09375 to 0.09375
- coefficients: float32 [192, 65536], P(None, 'feat'), may hold values from -3 to 3
- response: float32 [192, 4096], P(None, 'samp'), may hold values from -6 to 6
- active_set: int32 [192, 65536], P(None, 'feat'), may hold values 0 or 1
- lambda_path: float32 [192, 16], P('samp'), may hold values from 0.5 to 4
- lambda_index: int32 [192], P('samp'), may hold values from 1 to 15
Outputs:
- margins: float32 [192, 65536], P('samp', 'feat')
- peak_gradient: float32 [192], P('samp')
- violation: float32 [192], P('samp')
- screen_mass: float32 [192], P('samp')
Inputs may be any that keep to these rules, and one draw needn't show every extreme that they name: `active_set`: 1 marks a feature in the response's active set, 0 one outside it. `lambda_index`: the current point on the response's path; the previous point is the one just below it.
All inputs are finite; a program needn't handle non-finite values. No bound on the sum of `active_set` on one device may be relied on, other than what follows from the above.
Results may differ from a plain program's by a relative error of at most 0.000073.
Values sent between devices are 32-bit elements; how exact they have to be, the bound alone decides.
A program may use at most 128 MiB of HBM per device.

v0:
```python
import functools

import jax
import jax.numpy as jnp
from jax import lax
from jax.experimental import pallas as pl
from jax.experimental.pallas import tpu as pltpu
from jax.sharding import PartitionSpec as P

MESH = pl.DeviceIdType.MESH
F32 = jnp.float32
BF16 = jnp.bfloat16
CHUNK = 256
WIDE = 128
STEPS = 4
TILE = 256
PIECE = 32
SLOTS = 4
CROWS = 48


def split(v):
    hi = v.astype(BF16)
    return hi, (v - hi.astype(F32)).astype(BF16)


def nt(a, b):
    return lax.dot_general(a, b, (((1,), (1,)), ((), ())), preferred_element_type=F32)


def kernel(
    cfg,
    design, coef, active, response, path, index,
    margins, stats_out,
    parts, mm, stage, cst, ast, gb, crecv, xrecv, aown, pathv, indexv,
    part, yrecv, ysum, zrecv, full, resp, rr, sown, srecv,
    stage_sem, coef_sem, act_sem, resp_sem, aown_sem, path_sem, index_sem, out_sem,
    y_send, y_recv, z_send, z_recv, az_send, az_recv, ay_send, ay_recv,
    c_send, c_recv, x_send, x_recv, s_send, s_recv,
):
    S, F, A, B, X, R, rf, rp, rs, SL, FL = cfg
    Rp = F * rp
    C = SL // CHUNK
    V = CHUNK // WIDE
    T = FL // TILE
    KB = CHUNK // PIECE
    KW = FL // STEPS
    PS = KB // STEPS
    dh, dl = parts[:C], parts[C:]
    s = lax.axis_index("samp")
    f = lax.axis_index("feat")
    z = f // A
    y = f % A
    x = s // 2
    core = s % 2

    def padded(v):
        if rf == rp:
            return v
        fill = jnp.zeros((rp - rf, v.shape[1]), v.dtype)
        out = []
        for q in range(v.shape[0] // rf):
            out += [v[q * rf : (q + 1) * rf], fill]
        return jnp.concatenate(out, axis=0)

    barrier = pltpu.get_barrier_semaphore()
    peers = [(s, lax.rem(f + k, F)) for k in range(1, F)]
    peers += [(x * 2 + 1 - core, f)]
    peers += [(lax.rem(x + k, X) * 2 + core, f) for k in range(1, X)]
    for peer in peers:
        pl.semaphore_signal(barrier, inc=1, device_id=peer, device_id_type=MESH)

    half = FL // 2

    def coef_copies(i):
        rows = pl.ds((i // 2) * CROWS, CROWS)
        cols = pl.ds((i % 2) * half, half)
        return (
            pltpu.make_async_copy(coef.at[rows, cols], cst.at[i % 2], coef_sem.at[i % 2]),
            pltpu.make_async_copy(active.at[rows, cols], ast.at[i % 2], act_sem.at[i % 2]),
        )

    def piece_copy(p, slot):
        rows = pl.ds(pl.multiple_of(p * PIECE, PIECE), PIECE)
        return pltpu.make_async_copy(design.at[rows, :], stage.at[slot], stage_sem.at[slot])

    nc = 2 * R // CROWS
    NP = SL // PIECE
    for i in range(2):
        for cp in coef_copies(i):
            cp.start()
    for p in range(SLOTS):
        piece_copy(p, p).start()
    resp_copy = pltpu.make_async_copy(response, resp, resp_sem)
    path_copy = pltpu.make_async_copy(path, pathv, path_sem)
    index_copy = pltpu.make_async_copy(index, indexv, index_sem)
    for i in range(nc):
        for cp in coef_copies(i):
            cp.wait()
        m0 = (i // 2) * CROWS // rf * rp
        mr = CROWS // rf * rp
        step = 1024 if half % 1024 == 0 else half

        def mask_cols(j, carry, i=i, m0=m0, mr=mr, step=step):
            cols = pl.ds(pl.multiple_of(j * step, step), step)
            v = cst[i % 2, :, cols] * ast[i % 2, :, cols].astype(F32)
            hi, lo = split(padded(v))
            dst = pl.ds(pl.multiple_of((i % 2) * half + j * step, step), step)
            mm[m0 : m0 + mr, dst] = hi
            mm[Rp + m0 : Rp + m0 + mr, dst] = lo
            return carry

        lax.fori_loop(0, half // step, mask_cols, 0)
        if i + 2 < nc:
            for cp in coef_copies(i + 2):
                cp.start()
    resp_copy.start()
    path_copy.start()
    index_copy.start()
    own_first = pl.multiple_of(s * rs, 8)
    aown_copy = pltpu.make_async_copy(active.at[pl.ds(own_first, rs), :], aown, aown_sem)

    def split_piece(c, j):
        p = c * KB + j
        slot = lax.rem(p, SLOTS)
        piece_copy(p, slot).wait()
        rows = pl.ds(pl.multiple_of(j * PIECE, PIECE), PIECE)
        hi, lo = split(stage[slot])
        dh[c][rows, :] = hi
        dl[c][rows, :] = lo

    def next_piece(p):
        @pl.when(p + SLOTS < NP)
        def _():
            piece_copy(p + SLOTS, lax.rem(p, SLOTS)).start()

    def first_pieces(p, carry):
        split_piece(0, p)
        next_piece(p)
        return carry

    lax.fori_loop(0, KB, first_pieces, 0)
    pl.semaphore_wait(barrier, len(peers))

    def y_copy(c, k):
        to = lax.rem(y + k, A)
        return pltpu.make_async_remote_copy(
            part.at[c, to], yrecv.at[c, k - 1], y_send.at[c, k - 1], y_recv.at[c, k - 1],
            device_id=(s, z * A + to), device_id_type=MESH)

    def z_copy(c, k):
        to = lax.rem(z + k, B)
        return pltpu.make_async_remote_copy(
            ysum.at[c, to], zrecv.at[c, k - 1], z_send.at[c, k - 1], z_recv.at[c, k - 1],
            device_id=(s, to * A + y), device_id_type=MESH)

    def az_copy(c, k):
        to = lax.rem(z + k, B)
        return pltpu.make_async_remote_copy(
            full.at[c, y, z], full.at[c, y, z], az_send.at[c, k - 1], az_recv.at[c, k - 1],
            device_id=(s, to * A + y), device_id_type=MESH)

    def ay_copy(c, k):
        to = lax.rem(y + k, A)
        return pltpu.make_async_remote_copy(
            full.at[c, y], full.at[c, y], ay_send.at[c, k - 1], ay_recv.at[c, k - 1],
            device_id=(s, z * A + to), device_id_type=MESH)

    def stage1(c):
        for k in range(1, A):
            y_copy(c, k).start()

    def stage2(c):
        total = part[c, y]
        for k in range(1, A):
            y_copy(c, k).wait_recv()
            total = total + yrecv[c, k - 1]
        ysum[c] = total
        for k in range(1, B):
            z_copy(c, k).start()

    def stage3(c):
        total = ysum[c, z]
        for k in range(1, B):
            z_copy(c, k).wait_recv()
            total = total + zrecv[c, k - 1]
        full[c, y, z] = total
        for k in range(1, B):
            az_copy(c, k).start()

    def stage4(c):
        for k in range(1, B):
            az_copy(c, k).wait_recv()
        for k in range(1, A):
            ay_copy(c, k).start()

    def stage5(c):
        for k in range(1, A):
            ay_copy(c, k).wait_recv()
        cols = slice(c * WIDE, (c + 1) * WIDE)
        fitted = full[c].reshape(Rp, WIDE)
        hi, lo = split(padded(resp[:, cols]) - fitted)
        rr[0:Rp, cols] = hi
        rr[Rp : 2 * Rp, cols] = lo

    stages = (stage1, stage2, stage3, stage4, stage5)
    for c in range(C + 4):
        if c < C:
            def fit(j, acc, c=c):
                cols = pl.ds(pl.multiple_of(j * KW, KW), KW)
                if c + 1 < C:
                    for i in range(PS):
                        split_piece(c + 1, j * PS + i)
                both = nt(mm[:, cols], dh[c][:, cols])
                small = nt(mm[0:Rp, cols], dl[c][:, cols])
                if c + 1 < C:
                    for i in range(PS):
                        next_piece((c + 1) * KB + j * PS + i)
                return acc + (both[0:Rp] + (both[Rp:] + small))

            acc = lax.fori_loop(0, STEPS, fit, jnp.zeros((Rp, CHUNK), F32))
            for v in range(V):
                part[c * V + v] = acc[:, v * WIDE : (v + 1) * WIDE].reshape(A, B, rp, WIDE)
        if c == C - 1:
            aown_copy.start()
            resp_copy.wait()
        for n, g in enumerate(stages):
            if 0 <= c - n < C:
                for v in range(V):
                    g((c - n) * V + v)

    def c_copy(t):
        return pltpu.make_async_remote_copy(
            gb.at[t, 1 - core], crecv.at[t], c_send.at[t], c_recv.at[t],
            device_id=(x * 2 + 1 - core, f), device_id_type=MESH)

    def x_copy(t, k):
        to = lax.rem(x + k, X)
        return pltpu.make_async_remote_copy(
            gb.at[t, core, to], xrecv.at[t, k - 1], x_send.at[t, k - 1], x_recv.at[t, k - 1],
            device_id=(to * 2 + core, f), device_id_type=MESH)

    def forward(t):
        c_copy(t).wait_recv()
        gb[t, core] = gb[t, core] + crecv[t]
        for k in range(1, X):
            x_copy(t, k).start()

    def grad(t, carry):
        cols = pl.ds(pl.multiple_of(t * TILE, TILE), TILE)
        both = jnp.zeros((2 * Rp, TILE), F32)
        small = jnp.zeros((Rp, TILE), F32)
        for c in range(C):
            ks = slice(c * CHUNK, (c + 1) * CHUNK)
            both += jnp.dot(rr[:, ks], dh[c][:, cols], preferred_element_type=F32)
            small += jnp.dot(rr[0:Rp, ks], dl[c][:, cols], preferred_element_type=F32)
        g = both[0:Rp] + (both[Rp:] + small)
        if rf == rp:
            for o in range(S):
                gb[t, o % 2, o // 2] = g[o * rs : (o + 1) * rs]
        else:
            for q in range(F):
                o, r0 = q * rf // rs, q * rf % rs
                gb[t, o % 2, o // 2, r0 : r0 + rf, :] = g[q * rp : q * rp + rf]
        c_copy(t).start()

        @pl.when(t > 0)
        def _():
            forward(t - 1)

        return carry

    lax.fori_loop(0, T, grad, 0)
    forward(T - 1)
    aown_copy.wait()

    path_copy.wait()
    index_copy.wait()
    down = lax.broadcasted_iota(jnp.int32, (rs, rs), 0)
    across = lax.broadcasted_iota(jnp.int32, (rs, rs), 1)
    where = jnp.sum(jnp.where(down == across, indexv[...], 0), axis=1, keepdims=True)
    spots = lax.broadcasted_iota(jnp.int32, path.shape, 1)
    lam_new = jnp.sum(jnp.where(spots == where, pathv[...], 0.0), axis=1, keepdims=True)
    lam_old = jnp.sum(jnp.where(spots == where - 1, pathv[...], 0.0), axis=1, keepdims=True)
    threshold = 2.0 * lam_new - lam_old

    def out_copy(t):
        cols = pl.ds(pl.multiple_of(t * TILE, TILE), TILE)
        return pltpu.make_async_copy(xrecv.at[t, 0], margins.at[:, cols], out_sem.at[t])

    def finish(t, carry):
        peak, viol, mass = carry
        total = gb[t, core, x]
        for k in range(1, X):
            x_copy(t, k).wait_recv()
            total = total + xrecv[t, k - 1]
        cols = pl.ds(pl.multiple_of(t * TILE, TILE), TILE)
        mag = jnp.abs(total)
        mar = mag - threshold
        xrecv[t, 0] = mar
        out_copy(t).start()
        inactive = 1.0 - aown[:, cols].astype(F32)
        peak = jnp.maximum(peak, mag)
        viol = viol + inactive * jnp.maximum(mag - lam_new, 0.0)
        mass = mass + jnp.maximum(mar, 0.0)
        return peak, viol, mass

    zero = jnp.zeros((rs, TILE), F32)
    peak, viol, mass = lax.fori_loop(0, T, finish, (zero, zero, zero))
    lane = lax.broadcasted_iota(jnp.int32, (rs, 128), 1)
    peak = jnp.max(peak, axis=1, keepdims=True)
    viol = jnp.sum(viol, axis=1, keepdims=True)
    mass = jnp.sum(mass, axis=1, keepdims=True)
    mine = jnp.where(lane == 0, peak, jnp.where(lane == 1, viol, mass))
    sown[...] = mine

    def s_copy(k):
        return pltpu.make_async_remote_copy(
            sown, srecv.at[k - 1], s_send.at[k - 1], s_recv.at[k - 1],
            device_id=(s, lax.rem(f + k, F)), device_id_type=MESH)

    for k in range(1, F):
        s_copy(k).start()

    for c in range(C * V):
        for k in range(1, A):
            y_copy(c, k).wait_send()
            ay_copy(c, k).wait_send()
        for k in range(1, B):
            z_copy(c, k).wait_send()
            az_copy(c, k).wait_send()

    def drain(t, carry):
        c_copy(t).wait_send()
        for k in range(1, X):
            x_copy(t, k).wait_send()
        out_copy(t).wait()
        return carry

    lax.fori_loop(0, T, drain, 0)
    top, add = mine, mine
    for k in range(1, F):
        s_copy(k).wait_recv()
        top = jnp.maximum(top, srecv[k - 1])
        add = add + srecv[k - 1]
    stats_out[...] = jnp.where(lane == 0, top, add / (FL * F))
    for k in range(1, F):
        s_copy(k).wait_send()


def body(S, F, design, coefficients, response, active_set, lambda_path, lambda_index):
    SL, FL = design.shape
    R = coefficients.shape[0]
    rs = lambda_path.shape[0]
    A = 1
    while (2 * A) ** 2 <= F:
        A *= 2
    B = F // A
    X = S // 2
    rf = R // F
    rp = -(-rf // 8) * 8
    Rp = F * rp
    C, T, W = SL // CHUNK, FL // TILE, SL // WIDE
    cfg = (S, F, A, B, X, R, rf, rp, rs, SL, FL)
    hbm = pl.BlockSpec(memory_space=pl.ANY)
    vmem = pl.BlockSpec(memory_space=pltpu.VMEM)
    dma = pltpu.SemaphoreType.DMA
    margins, stats = pl.pallas_call(
        functools.partial(kernel, cfg),
        out_shape=(
            jax.ShapeDtypeStruct((rs, FL), F32),
            jax.ShapeDtypeStruct((rs, 128), F32),
        ),
        in_specs=[hbm] * 6,
        out_specs=(hbm, vmem),
        scratch_shapes=[
            [pltpu.VMEM((CHUNK, FL), BF16)] * (2 * C),
            pltpu.VMEM((2 * Rp, FL), BF16),
            pltpu.VMEM((SLOTS, PIECE, FL), F32),
            pltpu.VMEM((2, CROWS, FL // 2), F32),
            pltpu.VMEM((2, CROWS, FL // 2), jnp.int32),
            pltpu.VMEM((T, 2, X, rs, TILE), F32),
            pltpu.VMEM((T, X, rs, TILE), F32),
            pltpu.VMEM((T, max(X - 1, 1), rs, TILE), F32),
            pltpu.VMEM((rs, FL), jnp.int32),
            pltpu.VMEM(lambda_path.shape, F32),
            pltpu.VMEM((1, rs), jnp.int32),
            pltpu.VMEM((W, A, B, rp, WIDE), F32),
            pltpu.VMEM((W, A - 1, B, rp, WIDE), F32),
            pltpu.VMEM((W, B, rp, WIDE), F32),
            pltpu.VMEM((W, B - 1, rp, WIDE), F32),
            pltpu.VMEM((W, A, B, rp, WIDE), F32),
            pltpu.VMEM((R, SL), F32),
            pltpu.VMEM((2 * Rp, SL), BF16),
            pltpu.VMEM((rs, 128), F32),
            pltpu.VMEM((F - 1, rs, 128), F32),
            dma((SLOTS,)), dma((2,)), dma((2,)), dma, dma, dma, dma, dma((T,)),
            dma((W, A - 1)), dma((W, A - 1)), dma((W, B - 1)), dma((W, B - 1)),
            dma((W, B - 1)), dma((W, B - 1)), dma((W, A - 1)), dma((W, A - 1)),
            dma((T,)), dma((T,)), dma((T, X - 1)), dma((T, X - 1)),
            dma((F - 1,)), dma((F - 1,)),
        ],
        compiler_params=pltpu.CompilerParams(
            collective_id=0, has_side_effects=True, vmem_limit_bytes=67043328
        ),
    )(
        design, coefficients, active_set, response, lambda_path,
        lambda_index.reshape(1, rs),
    )
    return margins, stats[:, 0], stats[:, 1], stats[:, 2]


def solution(mesh):
    return jax.shard_map(
        functools.partial(body, mesh.shape["samp"], mesh.shape["feat"]),
        mesh=mesh,
        in_specs=(
            P("samp", "feat"),
            P(None, "feat"),
            P(None, "samp"),
            P(None, "feat"),
            P("samp", None),
            P("samp"),
        ),
        out_specs=(P("samp", "feat"), P("samp"), P("samp"), P("samp")),
        check_vma=False,
    )
```

profile of v0, /device:TPU:0, one launch (start us, length us, event | category | flops | bytes accessed | tf_op | source)
XLA Modules:
  0.0 102.8 jit_solution(1228244280280835671)
XLA Ops:
  0.6 1.4 %copy.11.path = f32[48,16]{1,0:T(8,128)} copy(f32[48,16]{0,1:T(8,128)} %param.10) | data formatting | bytes 6144 | tf_op args[4]
  2.0 96.5 %shard_map.93 = (f32[48,8192]{1,0:T(8,128)}, f32[48,128]{1,0:T(8,128)}) custom-call(f32[1024,8192]{1,0:T(8,128)} %design.1, f32[192,8192]{1,0:T(8,128)} %coef.1, s32[192,8192]{1,0:T(8,128)} %active.1, f32[192,1024]{1,0:T(8,128)} %response.1, f32[48,16]{1,0:T(8,128)} %copy.11.path, s32[1,48]{1,0:T(1,128)} %bitcast.1), custom_call_target="tpu_custom_call" | custom-call | tf_op jit(solution)/shard_map/pallas_call | solution.py:368
  98.5 1.6 %slice_reduce_fusion = (f32[48]{0:T(128)}, f32[48]{0:T(128)}, f32[48]{0:T(128)}) fusion(f32[48,128]{1,0:T(8,128)} %get-tuple-element.7), kind=kLoop, calls=%fused_computation | loop fusion | bytes 1152 | tf_op jit(solution)/shard_map/slice | solution.py:410
  100.1 2.7 %copy.13 = f32[48,8192]{1,0:T(8,128)} copy(f32[48,8192]{1,0:T(8,128)} %get-tuple-element.15) | data formatting | bytes 3145728
where the time goes:
time: 103 us
  Pallas kernels  96.5 us (94%)
  local copies, waits for them, and re-layouts  5.62 us (5%)
    pallas_call x1, Pallas kernels, body(): pl.pallas_call(functools.partial(kernel, cfg), out_shape=(jax.ShapeDtypeS...  96.5 us
    unnamed x2, local copies, waits for them, and re-layouts  4.03 us

commit v1 on v0

v1 whole, which is shorter than its diff:
```python
import functools

import jax
import jax.numpy as jnp
from jax import lax
from jax.experimental import pallas as pl
from jax.experimental.pallas import tpu as pltpu
from jax.sharding import PartitionSpec as P

MESH = pl.DeviceIdType.MESH
F32 = jnp.float32
BF16 = jnp.bfloat16
CHUNK = 256
KBLOCK = 1024
FLIGHT = 7
KSLICE = 256
TILE = 512
LAG = 2


def split(v):
    hi = v.astype(BF16)
    return hi, (v - hi.astype(F32)).astype(BF16)


def nt(a, b):
    return lax.dot_general(a, b, (((1,), (1,)), ((), ())), preferred_element_type=F32)


def nn(a, b):
    return jnp.dot(a, b, preferred_element_type=F32)


def pad8(n):
    return -(-n // 8) * 8


def kernel(
    cfg,
    design, coef, active, response, path, index,
    margins, stats_out,
    dsn, mm, gb, ast, crecv, xrecv, resp, pathv, indexv,
    part1, recv1, full1, rr1, part2, yrecv, ysum, zrecv, full2, rr2, sown, srecv, halves,
    design_sem, coef_sem, act_sem, resp_sem, path_sem, index_sem,
    d_send, d_recv, g_send, g_recv,
    y_send, y_recv, z_send, z_recv, az_send, az_recv, ay_send, ay_recv,
    c_send, c_recv, x_send, x_recv, s_send, s_recv,
):
    S, F, A, B, X, rs, SL, FL, groups = cfg
    C = SL // CHUNK
    NK = FL // KBLOCK
    T = FL // TILE
    (q1, f1, p1), (q2, f2, p2) = groups
    R1, R2 = F * p1, F * p2
    Rp = R1 + R2
    s = lax.axis_index("samp")
    f = lax.axis_index("feat")
    z = f // A
    y = f % A
    x = s // 2
    core = s % 2

    def padded(v, fg, pg):
        if fg == pg:
            return v
        fill = jnp.zeros((pg - fg, v.shape[1]), v.dtype)
        out = []
        for n in range(v.shape[0] // fg):
            out += [v[n * fg : (n + 1) * fg], fill]
        return jnp.concatenate(out, axis=0)

    barrier = pltpu.get_barrier_semaphore()
    peers = [(s, lax.rem(f + k, F)) for k in range(1, F)]
    peers += [(x * 2 + 1 - core, f)]
    peers += [(lax.rem(x + k, X) * 2 + core, f) for k in range(1, X)]
    for peer in peers:
        pl.semaphore_signal(barrier, inc=1, device_id=peer, device_id_type=MESH)

    def coef_copies(k):
        cols = pl.ds(k * KBLOCK, KBLOCK)
        out = []
        for o in range(S):
            rows = pl.ds(o * rs, rs)
            out.append(pltpu.make_async_copy(
                coef.at[rows, cols], gb.at[o % 2, o // 2, :, cols], coef_sem.at[k, o]))
            out.append(pltpu.make_async_copy(
                active.at[rows, cols], ast.at[o, :, cols], act_sem.at[k, o]))
        return out

    def design_copy(c, k):
        rows, cols = pl.ds(c * CHUNK, CHUNK), pl.ds(k * KBLOCK, KBLOCK)
        return pltpu.make_async_copy(
            design.at[rows, cols], dsn.at[rows, cols], design_sem.at[c, k])

    order = [(c, k) for c in range(C) for k in range(NK)]
    sent = [0]

    def load(upto):
        upto = min(upto, len(order))
        for c, k in order[sent[0] : upto]:
            if c == 0:
                for cp in coef_copies(k):
                    cp.start()
            design_copy(c, k).start()
        sent[0] = max(sent[0], upto)

    load(3)
    resp_copy = pltpu.make_async_copy(response, resp, resp_sem)
    path_copy = pltpu.make_async_copy(path, pathv, path_sem)
    index_copy = pltpu.make_async_copy(index, indexv, index_sem)

    def mask(k):
        with jax.named_scope(f'wc{k}'):
            for cp in coef_copies(k):
                cp.wait()
        step = 512

        def some(j, carry):
            cols = pl.ds(pl.multiple_of(k * KBLOCK + j * step, step), step)
            for o in range(S):
                v = gb[o % 2, o // 2, :, cols] * ast[o, :, cols].astype(F32)
                at, n = 0, 0
                for q, fg, pg in groups:
                    hi, lo = split(padded(v[at : at + q], fg, pg))
                    m0 = n + o * q // fg * pg
                    m1 = m0 + q // fg * pg
                    mm[m0:m1, cols] = hi
                    mm[Rp + m0 : Rp + m1, cols] = lo
                    at, n = at + q, n + F * pg
            return carry

        with jax.named_scope(f'mk{k}'):
            lax.fori_loop(0, KBLOCK // step, some, 0)

    def d_copy(c, k):
        to = lax.rem(f + k, F)
        return pltpu.make_async_remote_copy(
            part1.at[c, to], recv1.at[c, k - 1], d_send.at[c, k - 1], d_recv.at[c, k - 1],
            device_id=(s, to), device_id_type=MESH)

    def g_copy(c, k):
        to = lax.rem(f + k, F)
        return pltpu.make_async_remote_copy(
            full1.at[c, f], full1.at[c, f], g_send.at[c, k - 1], g_recv.at[c, k - 1],
            device_id=(s, to), device_id_type=MESH)

    def own_rows(g, c, block):
        q, fg, pg = groups[g]
        per = q // fg
        first = block // per * rs + (q1 if g else 0)
        which = lax.rem(block, per)
        cols = slice(c * CHUNK, (c + 1) * CHUNK)
        if fg % 8 == 0:
            return resp[pl.ds(pl.multiple_of(first + which * fg, 8), fg), cols]
        rows = resp[pl.ds(pl.multiple_of(first, 8), q), cols]
        v = rows[0:fg]
        for n in range(1, per):
            v = jnp.where(which == n, rows[n * fg : (n + 1) * fg], v)
        return padded(v, fg, pg)

    def keep(rr, rows, c, v):
        cols = slice(c * CHUNK, (c + 1) * CHUNK)
        hi, lo = split(v)
        rr[0:rows, cols] = hi
        rr[rows : 2 * rows, cols] = lo

    def one_send(c):
        for k in range(1, F):
            d_copy(c, k).start()

    def one_sum(c):
        total = part1[c, f]
        for k in range(1, F):
            d_copy(c, k).wait_recv()
            total = total + recv1[c, k - 1]
        full1[c, f] = own_rows(0, c, f) - total
        for k in range(1, F):
            g_copy(c, k).start()

    def one_keep(c):
        for k in range(1, F):
            g_copy(c, k).wait_recv()
        keep(rr1, R1, c, full1[c].reshape(R1, CHUNK))

    def y_copy(c, k):
        to = lax.rem(y + k, A)
        return pltpu.make_async_remote_copy(
            part2.at[c, to], yrecv.at[c, k - 1], y_send.at[c, k - 1], y_recv.at[c, k - 1],
            device_id=(s, z * A + to), device_id_type=MESH)

    def z_copy(c, k):
        to = lax.rem(z + k, B)
        return pltpu.make_async_remote_copy(
            ysum.at[c, to], zrecv.at[c, k - 1], z_send.at[c, k - 1], z_recv.at[c, k - 1],
            device_id=(s, to * A + y), device_id_type=MESH)

    def az_copy(c, k):
        to = lax.rem(z + k, B)
        return pltpu.make_async_remote_copy(
            full2.at[c, y, z], full2.at[c, y, z], az_send.at[c, k - 1], az_recv.at[c, k - 1],
            device_id=(s, to * A + y), device_id_type=MESH)

    def ay_copy(c, k):
        to = lax.rem(y + k, A)
        return pltpu.make_async_remote_copy(
            full2.at[c, y], full2.at[c, y], ay_send.at[c, k - 1], ay_recv.at[c, k - 1],
            device_id=(s, z * A + to), device_id_type=MESH)

    def two_y(c):
        for k in range(1, A):
            y_copy(c, k).start()

    def two_z(c):
        total = part2[c, y]
        for k in range(1, A):
            y_copy(c, k).wait_recv()
            total = total + yrecv[c, k - 1]
        ysum[c] = total
        for k in range(1, B):
            z_copy(c, k).start()

    def two_sum(c):
        total = ysum[c, z]
        for k in range(1, B):
            z_copy(c, k).wait_recv()
            total = total + zrecv[c, k - 1]
        full2[c, y, z] = own_rows(1, c, y * B + z) - total
        for k in range(1, B):
            az_copy(c, k).start()

    def two_back(c):
        for k in range(1, B):
            az_copy(c, k).wait_recv()
        for k in range(1, A):
            ay_copy(c, k).start()

    def two_keep(c):
        for k in range(1, A):
            ay_copy(c, k).wait_recv()
        keep(rr2, R2, c, full2[c].reshape(R2, CHUNK))

    def fit(c):
        rows = slice(c * CHUNK, (c + 1) * CHUNK)
        both = [jnp.zeros((2 * Rp, CHUNK), F32)] * 2
        small = [jnp.zeros((Rp, CHUNK), F32)] * 2
        for k in range(NK):
            if c == 0:
                mask(k)
            design_copy(c, k).wait()
            here = c * NK + k + 1
            load(here + (3 if here + 3 <= NK else FLIGHT))
            if here == NK:
                resp_copy.start()
                path_copy.start()
                index_copy.start()
            for j in range(KBLOCK // KSLICE):
                cols = slice(k * KBLOCK + j * KSLICE, k * KBLOCK + (j + 1) * KSLICE)
                hi, lo = split(dsn[rows, cols])
                both[j % 2] += nt(mm[:, cols], hi)
                small[j % 2] += nt(mm[0:Rp, cols], lo)
        for i in range(2):
            halves[i] = both[i][0:Rp] + (both[i][Rp:] + small[i])

        def join1(n, carry):
            at = pl.ds(pl.multiple_of(n * p1, p1), p1)
            part1[c, n] = halves[0, at] + halves[1, at]
            return carry

        def join2(n, carry):
            at = pl.ds(pl.multiple_of(R1 + n * p2, 8), p2)
            part2[c, n // B, n % B] = halves[0, at] + halves[1, at]
            return carry

        lax.fori_loop(0, F, join1, 0)
        lax.fori_loop(0, F, join2, 0)

    late = []
    early = []
    for c in range(C):
        with jax.named_scope(f"fit{c}"):
            fit(c)
        if c == 0:
            with jax.named_scope("bar"):
                pl.semaphore_wait(barrier, len(peers))
        with jax.named_scope(f"ar{c}"):
            one_send(c)
            if c < C - 2:
                two_y(c)
            if c == 2:
                resp_copy.wait()
            if c >= 2:
                one_sum(c - 2)
                if c - 2 < C - 2:
                    two_z(c - 2)
    with jax.named_scope("tail_a"):
        for c in range(max(C - 2, 0), C):
            with jax.named_scope(f"sum{c}"):
                one_sum(c)
            two_y(c)
    with jax.named_scope("tail_b"):
        for c in range(C):
            one_keep(c)

    def tile_at(t):
        return pl.ds(pl.multiple_of(t * TILE, TILE), TILE)

    def band(g):
        return pl.ds(q1, q2) if g else pl.ds(0, q1)

    def c_copy(g, t):
        return pltpu.make_async_remote_copy(
            gb.at[1 - core, :, band(g), tile_at(t)], crecv.at[:, band(g), tile_at(t)],
            c_send.at[g, t], c_recv.at[g, t],
            device_id=(x * 2 + 1 - core, f), device_id_type=MESH)

    def x_copy(g, t, k):
        to = lax.rem(x + k, X)
        return pltpu.make_async_remote_copy(
            gb.at[core, to, band(g), tile_at(t)], xrecv.at[k - 1, band(g), tile_at(t)],
            x_send.at[g, t, k - 1], x_recv.at[g, t, k - 1],
            device_id=(to * 2 + core, f), device_id_type=MESH)

    def forward(g, t):
        c_copy(g, t).wait_recv()
        at = (core, slice(None), band(g), tile_at(t))
        gb[at] = gb[at] + crecv[:, band(g), tile_at(t)]
        for k in range(1, X):
            x_copy(g, t, k).start()

    def grad(g, rr, t):
        q, fg, pg = groups[g]
        rows = F * pg
        cols = tile_at(t)
        both = jnp.zeros((2 * rows, TILE), F32)
        small = jnp.zeros((rows, TILE), F32)
        for c in range(C):
            ks = slice(c * CHUNK, (c + 1) * CHUNK)
            hi, lo = split(dsn[ks, cols])
            both += nn(rr[:, ks], hi)
            small += nn(rr[0:rows, ks], lo)
        v = both[0:rows] + (both[rows:] + small)
        for o in range(S):
            for n in range(q // fg):
                m0 = (o * (q // fg) + n) * pg
                r0 = (q1 if g else 0) + n * fg
                if fg == pg and n == 0:
                    gb[o % 2, o // 2, band(g), cols] = v[m0 : m0 + q]
                elif fg != pg:
                    gb[o % 2, o // 2, r0 : r0 + fg, cols] = v[m0 : m0 + fg]
        c_copy(g, t).start()

    def sweep(g, rr, lo, hi):
        def step(t, carry):
            grad(g, rr, t)

            @pl.when(t >= LAG)
            def _():
                forward(g, t - LAG)

            return carry

        lax.fori_loop(lo, hi, step, 0)

    def flush(g):
        for t in range(T - LAG, T):
            forward(g, t)

    rounds = []
    for c in range(max(C - 2, 0)):
        rounds.append([(two_sum, c)])
    rounds.append([(two_z, c) for c in range(max(C - 2, 0), C)])
    rounds.append([(two_back, c) for c in range(max(C - 2, 0))])
    rounds.append([(two_sum, c) for c in range(max(C - 2, 0), C)])
    rounds.append([(two_keep, c) for c in range(max(C - 2, 0))])
    rounds.append([(two_back, c) for c in range(max(C - 2, 0), C)])
    last = [(two_keep, c) for c in range(max(C - 2, 0), C)]
    n = len(rounds) + 1
    marks = [T * i // n for i in range(n + 1)]
    for i in range(n):
        with jax.named_scope(f"grad1_{i}"):
            sweep(0, rr1, marks[i], marks[i + 1])
        if i < len(rounds):
            with jax.named_scope(f"round{i}"):
                for fn, c in rounds[i]:
                    fn(c)
    with jax.named_scope("flush1"):
        flush(0)
    with jax.named_scope("last"):
        for fn, c in last:
            fn(c)
    with jax.named_scope("grad2"):
        sweep(1, rr2, 0, T)
    with jax.named_scope("flush2"):
        flush(1)

    path_copy.wait()
    index_copy.wait()
    diag = (lax.broadcasted_iota(jnp.int32, (rs, rs), 0)
            == lax.broadcasted_iota(jnp.int32, (rs, rs), 1))

    def column(row):
        return jnp.sum(jnp.where(diag, row, 0.0), axis=1, keepdims=True)

    def row(col):
        return jnp.sum(jnp.where(diag, col, 0.0), axis=0, keepdims=True)

    spots = lax.broadcasted_iota(jnp.int32, path.shape, 0)
    picked = indexv[...]
    lam_new = jnp.sum(jnp.where(spots == picked, pathv[...], 0.0), axis=0, keepdims=True)
    lam_old = jnp.sum(jnp.where(spots == picked - 1, pathv[...], 0.0), axis=0, keepdims=True)
    threshold = column(2.0 * lam_new - lam_old)
    lam_new = column(lam_new)

    def fold(v, op):
        out = v[:, 0:128]
        for i in range(1, TILE // 128):
            out = op(out, v[:, i * 128 : (i + 1) * 128])
        return out

    def finish(g):
        q, fg, pg = groups[g]
        at = band(g)
        lam = lam_new[q1:] if g else lam_new[:q1]
        thr = threshold[q1:] if g else threshold[:q1]

        def step(t, carry):
            peak, viol, mass = carry
            cols = tile_at(t)
            total = gb[core, x, at, cols]
            for k in range(1, X):
                x_copy(g, t, k).wait_recv()
                total = total + xrecv[k - 1, at, cols]
            mag = jnp.abs(total)
            mar = mag - thr
            margins[at, cols] = mar
            inactive = 1.0 - ast[s, at, cols].astype(F32)
            peak = jnp.maximum(peak, fold(mag, jnp.maximum))
            viol = viol + fold(inactive * jnp.maximum(mag - lam, 0.0), jnp.add)
            mass = mass + fold(jnp.maximum(mar, 0.0), jnp.add)
            return peak, viol, mass

        zero = jnp.zeros((q, 128), F32)
        return lax.fori_loop(0, T, step, (zero, zero, zero))

    with jax.named_scope("finish"):
        ends = [finish(g) for g in range(2)]
    tail = jax.named_scope("tail")
    tail.__enter__()
    peak, viol, mass = (jnp.concatenate([ends[0][i], ends[1][i]], axis=0) for i in range(3))
    peak = row(jnp.max(peak, axis=1, keepdims=True))
    viol = row(jnp.sum(viol, axis=1, keepdims=True))
    mass = row(jnp.sum(mass, axis=1, keepdims=True))
    mine = jnp.concatenate([peak, viol, mass, jnp.zeros((5, rs), F32)], axis=0)
    sown[:, 0:rs] = mine

    def s_copy(k):
        return pltpu.make_async_remote_copy(
            sown, srecv.at[k - 1], s_send.at[k - 1], s_recv.at[k - 1],
            device_id=(s, lax.rem(f + k, F)), device_id_type=MESH)

    for k in range(1, F):
        s_copy(k).start()

    for c in range(C):
        for k in range(1, F):
            d_copy(c, k).wait_send()
            g_copy(c, k).wait_send()
        for k in range(1, A):
            y_copy(c, k).wait_send()
            ay_copy(c, k).wait_send()
        for k in range(1, B):
            z_copy(c, k).wait_send()
            az_copy(c, k).wait_send()

    def drain(t, carry):
        for g in range(2):
            c_copy(g, t).wait_send()
            for k in range(1, X):
                x_copy(g, t, k).wait_send()
        return carry

    lax.fori_loop(0, T, drain, 0)
    top, add = mine, mine
    for k in range(1, F):
        s_copy(k).wait_recv()
        got = srecv[k - 1, :, 0:rs]
        top = jnp.maximum(top, got)
        add = add + got
    down = lax.broadcasted_iota(jnp.int32, (8, rs), 0)
    stats_out[:, 0:rs] = jnp.where(down == 0, top, add / (FL * F))
    for k in range(1, F):
        s_copy(k).wait_send()
    tail.__exit__(None, None, None)


def body(S, F, design, coefficients, response, active_set, lambda_path, lambda_index):
    SL, FL = design.shape
    R = coefficients.shape[0]
    rs, L = lambda_path.shape
    A = 1
    while (2 * A) ** 2 <= F:
        A *= 2
    B = F // A
    X = S // 2
    q1 = rs // 3
    groups = tuple((q, q * S // F, pad8(q * S // F)) for q in (q1, rs - q1))
    (q1, f1, p1), (q2, f2, p2) = groups
    R1, R2 = F * p1, F * p2
    C, T, NK = SL // CHUNK, FL // TILE, FL // KBLOCK
    cfg = (S, F, A, B, X, rs, SL, FL, groups)
    hbm = pl.BlockSpec(memory_space=pl.ANY)
    vmem = pl.BlockSpec(memory_space=pltpu.VMEM)
    dma = pltpu.SemaphoreType.DMA
    margins, stats = pl.pallas_call(
        functools.partial(kernel, cfg),
        out_shape=(
            jax.ShapeDtypeStruct((rs, FL), F32),
            jax.ShapeDtypeStruct((8, 128), F32),
        ),
        in_specs=[hbm] * 6,
        out_specs=(vmem, vmem),
        scratch_shapes=[
            pltpu.VMEM((SL, FL), F32),
            pltpu.VMEM((2 * (R1 + R2), FL), BF16),
            pltpu.VMEM((2, X, rs, FL), F32),
            pltpu.VMEM((S, rs, FL), jnp.int32),
            pltpu.VMEM((X, rs, FL), F32),
            pltpu.VMEM((max(X - 1, 1), rs, FL), F32),
            pltpu.VMEM((R, SL), F32),
            pltpu.VMEM((L, rs), F32),
            pltpu.VMEM((1, rs), jnp.int32),
            pltpu.VMEM((C, F, p1, CHUNK), F32),
            pltpu.VMEM((C, F - 1, p1, CHUNK), F32),
            pltpu.VMEM((C, F, p1, CHUNK), F32),
            pltpu.VMEM((2 * R1, SL), BF16),
            pltpu.VMEM((C, A, B, p2, CHUNK), F32),
            pltpu.VMEM((C, A - 1, B, p2, CHUNK), F32),
            pltpu.VMEM((C, B, p2, CHUNK), F32),
            pltpu.VMEM((C, B - 1, p2, CHUNK), F32),
            pltpu.VMEM((C, A, B, p2, CHUNK), F32),
            pltpu.VMEM((2 * R2, SL), BF16),
            pltpu.VMEM((8, 128), F32),
            pltpu.VMEM((F - 1, 8, 128), F32),
            pltpu.VMEM((2, R1 + R2, CHUNK), F32),
            dma((C, NK)), dma((NK, S)), dma((NK, S)), dma, dma, dma,
            dma((C, F - 1)), dma((C, F - 1)), dma((C, F - 1)), dma((C, F - 1)),
            dma((C, A - 1)), dma((C, A - 1)), dma((C, B - 1)), dma((C, B - 1)),
            dma((C, B - 1)), dma((C, B - 1)), dma((C, A - 1)), dma((C, A - 1)),
            dma((2, T)), dma((2, T)), dma((2, T, X - 1)), dma((2, T, X - 1)),
            dma((F - 1,)), dma((F - 1,)),
        ],
        compiler_params=pltpu.CompilerParams(
            collective_id=0, has_side_effects=True, vmem_limit_bytes=67043328
        ),
    )(
        design, coefficients, active_set, response, lambda_path.T,
        lambda_index.reshape(1, rs),
    )
    return margins, stats[0, :rs], stats[1, :rs], stats[2, :rs]


def solution(mesh):
    return jax.shard_map(
        functools.partial(body, mesh.shape["samp"], mesh.shape["feat"]),
        mesh=mesh,
        in_specs=(
            P("samp", "feat"),
            P(None, "feat"),
            P(None, "samp"),
            P(None, "feat"),
            P("samp", None),
            P("samp"),
        ),
        out_specs=(P("samp", "feat"), P("samp"), P("samp"), P("samp")),
        check_vma=False,
    )
```

time: 103 us -> 89.6 us (0.87)
  Pallas kernels: 96.5 us -> 84.8 us
  local copies, waits for them, and re-layouts: 5.62 us -> 3.95 us
    pallas_call x1, Pallas kernels: 96.5 us -> 84.8 us  [body(): pl.pallas_call(functools.partial(kernel, cfg), out_shape=(jax.ShapeDtypeS...]
    slice x1 -> x0, local copies, waits for them, and re-layouts: 1.59 us -> none  [body(): return (margins, stats[:, 0], stats[:, 1], stats[:, 2])]
    unnamed x2 -> x1, local copies, waits for them, and re-layouts: 4.03 us -> 2.65 us
    squeeze x0 -> x1, local copies, waits for them, and re-layouts: none -> 1.3 us  [body(): return (margins, stats[0, :rs], stats[1, :rs], stats[2, :rs])]
where the time goes in v1:
time: 89.6 us; the launch traced here: 89.4 us
  Pallas kernels  84.8 us (95%)
  local copies, waits for them, and re-layouts  3.95 us (4%)
    pallas_call x1, Pallas kernels, body(): pl.pallas_call(functools.partial(kernel, cfg), out_shape=(jax.ShapeDtypeS...  84.8 us
    unnamed x1, local copies, waits for them, and re-layouts  2.65 us

profile of v1, /device:TPU:0, one launch (start us, length us, event | category | flops | bytes accessed | tf_op | source)
XLA Modules:
  0.0 89.4 jit_solution(15586144442447115862)
XLA Ops:
  0.6 84.8 %shard_map.93 = (f32[48,8192]{1,0:T(8,128)}, f32[8,128]{1,0:T(8,128)}) custom-call(f32[1024,8192]{1,0:T(8,128)} %design.1, f32[192,8192]{1,0:T(8,128)} %coef.1, s32[192,8192]{1,0:T(8,128)} %active.1, f32[192,1024]{1,0:T(8,128)} %response.1, f32[16,48]{1,0:T(8,128)} %bitcast.8, s32[1,48]{1,0:T(1,128)} %bitcast.9), custom_call_target="tpu_custom_call" | custom-call | tf_op jit(solution)/shard_map/pallas_call | solution.py:514
  85.5 1.3 %slice_bitcast_fusion = (f32[48]{0:T(128)}, f32[48]{0:T(128)}, f32[48]{0:T(128)}) fusion(f32[8,128]{1,0:T(8,128)} %get-tuple-element.7), kind=kLoop, calls=%fused_computation | loop fusion | bytes 1152 | tf_op jit(solution)/shard_map/squeeze | solution.py:559
  86.8 2.7 %copy.11 = f32[48,8192]{1,0:T(8,128)} copy(f32[48,8192]{1,0:T(8,128)} %get-tuple-element.15) | data formatting | bytes 3145728

commit v2 on v1

v2 whole, which is shorter than its diff:
```python
import functools

import jax
import jax.numpy as jnp
from jax import lax
from jax.experimental import pallas as pl
from jax.experimental.pallas import tpu as pltpu
from jax.sharding import PartitionSpec as P

MESH = pl.DeviceIdType.MESH
F32 = jnp.float32
BF16 = jnp.bfloat16
CHUNK = 256
KBLOCK = 1024
RING = 4
PARTS = 3
CUTS = 4
KSLICE = 512
TILE = 512
LAG = 2


def split(v):
    hi = v.astype(BF16)
    return hi, (v - hi.astype(F32)).astype(BF16)


def nt(a, b):
    return lax.dot_general(a, b, (((1,), (1,)), ((), ())), preferred_element_type=F32)


def nn(a, b):
    return jnp.dot(a, b, preferred_element_type=F32)


def pad8(n):
    return -(-n // 8) * 8


def kernel(
    cfg,
    design, coef, active, response, path, index,
    margins, stats_out,
    dsn, mm, gb, ast, crecv, xrecv, resp, pathv, indexv,
    part, recv, full, rr, halves, sown, srecv,
    design_sem, chunk_sem, coef_sem, act_sem, resp_sem, path_sem, index_sem,
    d_send, d_recv, g_send, g_recv,
    c_send, c_recv, x_send, x_recv, s_send, s_recv,
):
    S, F, X, rs, SL, FL, groups = cfg
    C = SL // CHUNK
    NK = FL // KBLOCK
    T = FL // TILE
    G = len(groups)
    first = [sum(q for q, fg, pg in groups[:g]) for g in range(G)]
    base = [sum(F * pg for q, fg, pg in groups[:g]) for g in range(G)]
    Rp = sum(F * pg for q, fg, pg in groups)
    s = lax.axis_index("samp")
    f = lax.axis_index("feat")
    x = s // 2
    core = s % 2

    def padded(v, fg, pg):
        if fg == pg:
            return v
        fill = jnp.zeros((pg - fg, v.shape[1]), v.dtype)
        out = []
        for n in range(v.shape[0] // fg):
            out += [v[n * fg : (n + 1) * fg], fill]
        return jnp.concatenate(out, axis=0)

    barrier = pltpu.get_barrier_semaphore()
    peers = [(s, lax.rem(f + k, F)) for k in range(1, F)]
    peers += [(x * 2 + 1 - core, f)]
    peers += [(lax.rem(x + k, X) * 2 + core, f) for k in range(1, X)]
    for peer in peers:
        pl.semaphore_signal(barrier, inc=1, device_id=peer, device_id_type=MESH)

    def coef_copies(k):
        cols = pl.ds(k * KBLOCK, KBLOCK)
        return (
            pltpu.make_async_copy(
                coef.at[:, :, :, cols], gb.at[:, :, :, cols], coef_sem.at[k % RING]),
            pltpu.make_async_copy(active.at[:, :, cols], ast.at[:, :, cols], act_sem.at[k % RING]),
        )

    def first_copy(k):
        cols = pl.ds(k * KBLOCK, KBLOCK)
        rows = pl.ds(0, CHUNK)
        return pltpu.make_async_copy(
            design.at[rows, cols], dsn.at[rows, cols], design_sem.at[k % RING])

    def chunk_copy(c, n):
        rows = pl.ds(c * CHUNK, CHUNK)
        cols = pl.ds(n * (FL // CUTS), FL // CUTS)
        return pltpu.make_async_copy(
            design.at[rows, cols], dsn.at[rows, cols], chunk_sem.at[c % 2, n])

    def load(k):
        if k < NK:
            for cp in coef_copies(k):
                cp.start()
            first_copy(k).start()
        elif C > 1 and k - NK < CUTS:
            chunk_copy(1, k - NK).start()

    for k in range(3):
        load(k)
    resp_copy = pltpu.make_async_copy(response, resp, resp_sem)
    path_copy = pltpu.make_async_copy(path, pathv, path_sem)
    index_copy = pltpu.make_async_copy(index, indexv, index_sem)

    def mask(k):
        for cp in coef_copies(k):
            cp.wait()
        step = 512

        def some(j, carry):
            cols = pl.ds(pl.multiple_of(k * KBLOCK + j * step, step), step)
            for o in range(S):
                v = gb[o // 2, o % 2, :, cols] * ast[o, :, cols].astype(F32)
                at, n = 0, 0
                for q, fg, pg in groups:
                    hi, lo = split(padded(v[at : at + q], fg, pg))
                    m0 = n + o * q // fg * pg
                    m1 = m0 + q // fg * pg
                    mm[m0:m1, cols] = hi
                    mm[Rp + m0 : Rp + m1, cols] = lo
                    at, n = at + q, n + F * pg
            return carry

        lax.fori_loop(0, KBLOCK // step, some, 0)

    def all_bytes(ref, sem):
        pltpu.make_async_copy(ref, ref, sem).wait()

    def d_copy(g, c, k):
        to = lax.rem(f + k, F)
        return pltpu.make_async_remote_copy(
            part[g].at[c, to], recv[g].at[c, k - 1], d_send.at[g], d_recv.at[g, c],
            device_id=(s, to), device_id_type=MESH)

    def g_copy(g, c, k):
        to = lax.rem(f + k, F)
        return pltpu.make_async_remote_copy(
            full[g].at[c, f], full[g].at[c, f], g_send.at[g], g_recv.at[g, c],
            device_id=(s, to), device_id_type=MESH)

    def own_rows(g, c, block):
        q, fg, pg = groups[g]
        per = q // fg
        start = block // per * rs + first[g]
        which = lax.rem(block, per)
        cols = slice(c * CHUNK, (c + 1) * CHUNK)
        if fg % 8 == 0:
            return resp[pl.ds(pl.multiple_of(start + which * fg, 8), fg), cols]
        rows = resp[pl.ds(pl.multiple_of(start, 8), q), cols]
        v = rows[0:fg]
        for n in range(1, per):
            v = jnp.where(which == n, rows[n * fg : (n + 1) * fg], v)
        return padded(v, fg, pg)

    def send(g, c):
        for k in range(1, F):
            d_copy(g, c, k).start()

    def total(g, c):
        all_bytes(recv[g].at[c], d_recv.at[g, c])
        v = part[g][c, f]
        for k in range(1, F):
            v = v + recv[g][c, k - 1]
        full[g][c, f] = own_rows(g, c, f) - v
        for k in range(1, F):
            g_copy(g, c, k).start()

    def keep(g, c):
        all_bytes(recv[g].at[c], g_recv.at[g, c])
        rows = F * groups[g][2]
        cols = slice(c * CHUNK, (c + 1) * CHUNK)
        hi, lo = split(full[g][c].reshape(rows, CHUNK))
        rr[g][0:rows, cols] = hi
        rr[g][rows : 2 * rows, cols] = lo

    def fit(c, middle):
        rows = slice(c * CHUNK, (c + 1) * CHUNK)
        both = [jnp.zeros((2 * Rp, CHUNK), F32)] * 2
        small = [jnp.zeros((Rp, CHUNK), F32)] * 2
        if c > 1:
            for n in range(CUTS):
                chunk_copy(c, n).wait()
            if c + 1 < C:
                for n in range(CUTS):
                    chunk_copy(c + 1, n).start()
        for k in range(NK):
            if c == 0:
                mask(k)
                first_copy(k).wait()
                load(k + 3)
            if c == 1 and k % (NK // CUTS) == 0:
                n = k // (NK // CUTS)
                chunk_copy(1, n).wait()
                load(NK + 3 + n)
                if C > 2:
                    chunk_copy(2, n).start()
            for j in range(KBLOCK // KSLICE):
                cols = slice(k * KBLOCK + j * KSLICE, k * KBLOCK + (j + 1) * KSLICE)
                hi, lo = split(dsn[rows, cols])
                both[j % 2] += nt(mm[:, cols], hi)
                small[j % 2] += nt(mm[0:Rp, cols], lo)
            if k == NK // 2 - 1:
                middle(c)
        for i in range(2):
            halves[i] = both[i][0:Rp] + (both[i][Rp:] + small[i])
        if c == 0:
            resp_copy.start()
            path_copy.start()
            index_copy.start()
            pl.semaphore_wait(barrier, len(peers))
        for g, (q, fg, pg) in enumerate(groups):
            def join(n, carry, g=g, pg=pg):
                at = pl.ds(pl.multiple_of(base[g] + n * pg, 8), pg)
                part[g][c, n] = halves[0, at] + halves[1, at]
                return carry

            lax.fori_loop(0, F, join, 0)
            if g == 0 or (g == 1 and c < C - 1):
                send(g, c)

    def middle(c):
        if c == min(2, C - 1):
            resp_copy.wait()
        if c >= 2:
            total(0, c - 2)

    for c in range(C):
        with jax.named_scope(f"fit{c}"):
            fit(c, middle)
    end = C - 1
    with jax.named_scope("sum2"):
        for c in range(max(C - 2, 0), end):
            total(0, c)
    with jax.named_scope("early"):
        for g in range(1, min(2, G)):
            for c in range(max(C - 2, 0)):
                total(g, c)
    with jax.named_scope("sum3"):
        total(0, end)
    with jax.named_scope("early2"):
        for g in range(1, min(2, G)):
            send(g, end)
            for c in range(max(C - 2, 0), end):
                total(g, c)
    for c in range(C):
        with jax.named_scope(f"keep{c}"):
            keep(0, c)

    def tile_at(t):
        return pl.ds(pl.multiple_of(t * TILE, TILE), TILE)

    def band(g):
        return pl.ds(first[g], groups[g][0])

    def c_copy(g, t):
        return pltpu.make_async_remote_copy(
            gb.at[:, 1 - core, band(g), tile_at(t)], crecv.at[:, band(g), tile_at(t)],
            c_send, c_recv.at[g, t],
            device_id=(x * 2 + 1 - core, f), device_id_type=MESH)

    def x_copy(g, t, k):
        to = lax.rem(x + k, X)
        return pltpu.make_async_remote_copy(
            gb.at[to, core, band(g), tile_at(t)], xrecv.at[k - 1, band(g), tile_at(t)],
            x_send, x_recv.at[g, t],
            device_id=(to * 2 + core, f), device_id_type=MESH)

    def forward(g, t):
        c_copy(g, t).wait_recv()
        at = (slice(None), core, band(g), tile_at(t))
        gb[at] = gb[at] + crecv[:, band(g), tile_at(t)]
        for k in range(1, X):
            x_copy(g, t, k).start()

    def grad(g, res, t):
        q, fg, pg = groups[g]
        rows = F * pg
        cols = tile_at(t)
        both = jnp.zeros((2 * rows, TILE), F32)
        small = jnp.zeros((rows, TILE), F32)
        for c in range(C):
            ks = slice(c * CHUNK, (c + 1) * CHUNK)
            hi, lo = split(dsn[ks, cols])
            both += nn(res[:, ks], hi)
            small += nn(res[0:rows, ks], lo)
        v = both[0:rows] + (both[rows:] + small)
        for o in range(S):
            for n in range(q // fg):
                m0 = (o * (q // fg) + n) * pg
                r0 = first[g] + n * fg
                if fg == pg and n == 0:
                    gb[o // 2, o % 2, band(g), cols] = v[m0 : m0 + q]
                elif fg != pg:
                    gb[o // 2, o % 2, r0 : r0 + fg, cols] = v[m0 : m0 + fg]
        c_copy(g, t).start()

    def sweep(g, res, lo, hi):
        def step(t, carry):
            grad(g, res, t)

            @pl.when(t >= LAG)
            def _():
                forward(g, t - LAG)

            return carry

        lax.fori_loop(lo, hi, step, 0)

    def flush(g):
        for t in range(T - LAG, T):
            forward(g, t)

    for g in range(G):
        mark = 2 * T // 16
        with jax.named_scope(f"grad{g}_0"):
            sweep(g, rr[g], 0, mark)
        with jax.named_scope(f"round{g}"):
            if g + 1 < G:
                if g == 0:
                    total(1, end)
                if g + 2 < G:
                    for c in range(C):
                        send(g + 2, c)
        with jax.named_scope(f"grad{g}_1"):
            sweep(g, rr[g], mark, T)
            flush(g)
        with jax.named_scope(f"last{g}"):
            for c in range(C):
                if g + 1 < G:
                    keep(g + 1, c)
                if g + 2 < G:
                    total(g + 2, c)

    path_copy.wait()
    index_copy.wait()
    diag = (lax.broadcasted_iota(jnp.int32, (rs, rs), 0)
            == lax.broadcasted_iota(jnp.int32, (rs, rs), 1))

    def column(row):
        return jnp.sum(jnp.where(diag, row, 0.0), axis=1, keepdims=True)

    def row(col):
        return jnp.sum(jnp.where(diag, col, 0.0), axis=0, keepdims=True)

    spots = lax.broadcasted_iota(jnp.int32, path.shape, 0)
    picked = indexv[...]
    lam_new = jnp.sum(jnp.where(spots == picked, pathv[...], 0.0), axis=0, keepdims=True)
    lam_old = jnp.sum(jnp.where(spots == picked - 1, pathv[...], 0.0), axis=0, keepdims=True)
    threshold = column(2.0 * lam_new - lam_old)
    lam_new = column(lam_new)

    def fold(v, op):
        out = v[:, 0:128]
        for i in range(1, TILE // 128):
            out = op(out, v[:, i * 128 : (i + 1) * 128])
        return out

    def finish(g):
        q, fg, pg = groups[g]
        at = band(g)
        lam = lam_new[first[g] : first[g] + q]
        thr = threshold[first[g] : first[g] + q]

        def step(t, carry):
            peak, viol, mass = carry
            cols = tile_at(t)
            all_bytes(xrecv.at[:, at, cols], x_recv.at[g, t])
            total = gb[x, core, at, cols]
            for k in range(1, X):
                total = total + xrecv[k - 1, at, cols]
            mag = jnp.abs(total)
            mar = mag - thr
            margins[at, cols] = mar
            inactive = 1.0 - ast[s, at, cols].astype(F32)
            peak = jnp.maximum(peak, fold(mag, jnp.maximum))
            viol = viol + fold(inactive * jnp.maximum(mag - lam, 0.0), jnp.add)
            mass = mass + fold(jnp.maximum(mar, 0.0), jnp.add)
            return peak, viol, mass

        zero = jnp.zeros((q, 128), F32)
        return lax.fori_loop(0, T, step, (zero, zero, zero))

    with jax.named_scope("finish"):
        ends = [finish(g) for g in range(G)]
    tail = jax.named_scope("tail")
    tail.__enter__()
    peak, viol, mass = (jnp.concatenate([e[i] for e in ends], axis=0) for i in range(3))
    peak = row(jnp.max(peak, axis=1, keepdims=True))
    viol = row(jnp.sum(viol, axis=1, keepdims=True))
    mass = row(jnp.sum(mass, axis=1, keepdims=True))
    mine = jnp.concatenate([peak, viol, mass, jnp.zeros((5, rs), F32)], axis=0)
    sown[:, 0:rs] = mine

    def s_copy(k):
        return pltpu.make_async_remote_copy(
            sown, srecv.at[k - 1], s_send, s_recv,
            device_id=(s, lax.rem(f + k, F)), device_id_type=MESH)

    for k in range(1, F):
        s_copy(k).start()

    for g in range(G):
        all_bytes(recv[g], d_send.at[g])
        all_bytes(recv[g], g_send.at[g])
    all_bytes(crecv, c_send)
    all_bytes(xrecv, x_send)
    all_bytes(srecv, s_recv)
    top, add = mine, mine
    for k in range(1, F):
        got = srecv[k - 1, :, 0:rs]
        top = jnp.maximum(top, got)
        add = add + got
    down = lax.broadcasted_iota(jnp.int32, (8, rs), 0)
    stats_out[:, 0:rs] = jnp.where(down == 0, top, add / (FL * F))
    all_bytes(srecv, s_send)
    tail.__exit__(None, None, None)


def body(S, F, design, coefficients, response, active_set, lambda_path, lambda_index):
    SL, FL = design.shape
    R = coefficients.shape[0]
    rs, L = lambda_path.shape
    X = S // 2
    parts = PARTS if rs % (8 * PARTS) == 0 else 1
    q = rs // parts
    groups = ((q, q * S // F, pad8(q * S // F)),) * parts
    Rp = sum(F * pg for q, fg, pg in groups)
    C, T = SL // CHUNK, FL // TILE
    cfg = (S, F, X, rs, SL, FL, groups)
    hbm = pl.BlockSpec(memory_space=pl.ANY)
    vmem = pl.BlockSpec(memory_space=pltpu.VMEM)
    dma = pltpu.SemaphoreType.DMA
    margins, stats = pl.pallas_call(
        functools.partial(kernel, cfg),
        out_shape=(
            pltpu.VMEM((rs, FL), F32),
            pltpu.VMEM((8, 128), F32),
        ),
        in_specs=[hbm] * 6,
        out_specs=(vmem, vmem),
        scratch_shapes=[
            pltpu.VMEM((SL, FL), F32),
            pltpu.VMEM((2 * Rp, FL), BF16),
            pltpu.VMEM((X, 2, rs, FL), F32),
            pltpu.VMEM((S, rs, FL), jnp.int32),
            pltpu.VMEM((X, rs, FL), F32),
            pltpu.VMEM((max(X - 1, 1), rs, FL), F32),
            pltpu.VMEM((R, SL), F32),
            pltpu.VMEM((L, rs), F32),
            pltpu.VMEM((1, rs), jnp.int32),
            [pltpu.VMEM((C, F, p, CHUNK), F32) for q, fg, p in groups],
            [pltpu.VMEM((C, F - 1, p, CHUNK), F32) for q, fg, p in groups],
            [pltpu.VMEM((C, F, p, CHUNK), F32) for q, fg, p in groups],
            [pltpu.VMEM((2 * F * p, SL), BF16) for q, fg, p in groups],
            pltpu.VMEM((2, Rp, CHUNK), F32),
            pltpu.VMEM((8, 128), F32),
            pltpu.VMEM((F - 1, 8, 128), F32),
            dma((RING,)), dma((2, CUTS)), dma((RING,)), dma((RING,)), dma, dma, dma,
            dma((parts,)), dma((parts, C)), dma((parts,)), dma((parts, C)),
            dma, dma((parts, T)), dma, dma((parts, T)), dma, dma,
        ],
        compiler_params=pltpu.CompilerParams(
            collective_id=0, has_side_effects=True, vmem_limit_bytes=64880640
        ),
    )(
        design, coefficients.reshape(X, 2, rs, FL), active_set.reshape(S, rs, FL), response, lambda_path.T,
        lambda_index.reshape(1, rs),
    )
    return margins, stats[0, :rs], stats[1, :rs], stats[2, :rs]


def solution(mesh):
    return jax.shard_map(
        functools.partial(body, mesh.shape["samp"], mesh.shape["feat"]),
        mesh=mesh,
        in_specs=(
            P("samp", "feat"),
            P(None, "feat"),
            P(None, "samp"),
            P(None, "feat"),
            P("samp", None),
            P("samp"),
        ),
        out_specs=(P("samp", "feat"), P("samp"), P("samp"), P("samp")),
        check_vma=False,
    )
```

time: 89.6 us -> 79.8 us (0.89)
  Pallas kernels: 84.8 us -> 77.4 us
  local copies, waits for them, and re-layouts: 3.95 us -> 1.66 us
    pallas_call x1, Pallas kernels: 84.8 us -> 77.4 us  [body(): pl.pallas_call(functools.partial(kernel, cfg), out_shape=(pltpu.VMEM((rs,...]
    unnamed x1, local copies, waits for them, and re-layouts: 2.65 us -> 1.14 us
where the time goes in v2:
time: 79.8 us; the launch traced here: 79.7 us
  Pallas kernels  77.4 us (97%)
  local copies, waits for them, and re-layouts  1.66 us (2%)
    pallas_call x1, Pallas kernels, body(): pl.pallas_call(functools.partial(kernel, cfg), out_shape=(pltpu.VMEM((rs,...  77.4 us

profile of v2, /device:TPU:0, one launch (start us, length us, event | category | flops | bytes accessed | tf_op | source)
XLA Modules:
  0.0 79.7 jit_solution(16090829401455112948)
XLA Ops:
  0.6 77.4 %shard_map.93 = (f32[48,8192]{1,0:T(8,128)S(1)}, f32[8,128]{1,0:T(8,128)S(1)}) custom-call(f32[1024,8192]{1,0:T(8,128)} %design.1, f32[2,2,48,8192]{3,2,1,0:T(8,128)} %bitcast.10, s32[4,48,8192]{2,1,0:T(8,128)} %bitcast.11, f32[192,1024]{1,0:T(8,128)} %response.1, f32[16,48]{1,0:T(8,128)} %bitcast.12, s32[1,48]{1,0:T(1,128)} %bitcast.13), custom_call_target="tpu_custom_call" | custom-call | tf_op jit(solution)/shard_map/pallas_call | solution.py:441
  78.0 0.5 slice_bitcast_fusion
  78.5 1.1 %copy.11 = f32[48,8192]{1,0:T(8,128)} copy(f32[48,8192]{1,0:T(8,128)S(1)} %get-tuple-element.11) | data formatting | bytes 3145728

commit v3 on v2

--- a/solution.py
+++ b/solution.py
@@ -15,6 +15,7 @@
 RING = 4
 PARTS = 3
 CUTS = 4
+HEAD = 2
 KSLICE = 512
 TILE = 512
 LAG = 2
@@ -86,7 +87,7 @@
 
     def first_copy(k):
         cols = pl.ds(k * KBLOCK, KBLOCK)
-        rows = pl.ds(0, CHUNK)
+        rows = pl.ds(0, HEAD * CHUNK)
         return pltpu.make_async_copy(
             design.at[rows, cols], dsn.at[rows, cols], design_sem.at[k % RING])
 
@@ -101,10 +102,10 @@
             for cp in coef_copies(k):
                 cp.start()
             first_copy(k).start()
-        elif C > 1 and k - NK < CUTS:
-            chunk_copy(1, k - NK).start()
-
-    for k in range(3):
+        elif C > HEAD and k - NK < CUTS:
+            chunk_copy(HEAD, k - NK).start()
+
+    for k in range(2):
         load(k)
     resp_copy = pltpu.make_async_copy(response, resp, resp_sem)
     path_copy = pltpu.make_async_copy(path, pathv, path_sem)
@@ -181,41 +182,62 @@
         rr[g][0:rows, cols] = hi
         rr[g][rows : 2 * rows, cols] = lo
 
-    def fit(c, middle):
+    def slices(k):
+        for j in range(KBLOCK // KSLICE):
+            yield j, slice(k * KBLOCK + j * KSLICE, k * KBLOCK + (j + 1) * KSLICE)
+
+    def fit_head():
+        both = [jnp.zeros((2 * Rp, CHUNK), F32)] * HEAD
+        small = [jnp.zeros((Rp, CHUNK), F32)] * HEAD
+        for k in range(NK):
+            mask(k)
+            first_copy(k).wait()
+            if k == 0:
+                load(2)
+            load(k + 3)
+            for j, cols in slices(k):
+                for c in range(HEAD):
+                    hi, lo = split(dsn[c * CHUNK : (c + 1) * CHUNK, cols])
+                    both[c] += nt(mm[:, cols], hi)
+                    small[c] += nt(mm[0:Rp, cols], lo)
+        resp_copy.start()
+        path_copy.start()
+        index_copy.start()
+        accs = [both[c][0:Rp] + (both[c][Rp:] + small[c]) for c in range(HEAD)]
+        pl.semaphore_wait(barrier, len(peers))
+        for g in range(min(2, G)):
+            rows = F * groups[g][2]
+            for c in range(HEAD):
+                part[g][c] = accs[c][base[g] : base[g] + rows].reshape(F, groups[g][2], CHUNK)
+                send(g, c)
+        for g in range(2, G):
+            rows = F * groups[g][2]
+            for c in range(HEAD):
+                part[g][c] = accs[c][base[g] : base[g] + rows].reshape(F, groups[g][2], CHUNK)
+
+    def fit(c):
         rows = slice(c * CHUNK, (c + 1) * CHUNK)
         both = [jnp.zeros((2 * Rp, CHUNK), F32)] * 2
         small = [jnp.zeros((Rp, CHUNK), F32)] * 2
-        if c > 1:
+        if c > HEAD:
             for n in range(CUTS):
                 chunk_copy(c, n).wait()
             if c + 1 < C:
                 for n in range(CUTS):
                     chunk_copy(c + 1, n).start()
         for k in range(NK):
-            if c == 0:
-                mask(k)
-                first_copy(k).wait()
-                load(k + 3)
-            if c == 1 and k % (NK // CUTS) == 0:
+            if c == HEAD and k % (NK // CUTS) == 0:
                 n = k // (NK // CUTS)
-                chunk_copy(1, n).wait()
+                chunk_copy(c, n).wait()
                 load(NK + 3 + n)
-                if C > 2:
-                    chunk_copy(2, n).start()
-            for j in range(KBLOCK // KSLICE):
-                cols = slice(k * KBLOCK + j * KSLICE, k * KBLOCK + (j + 1) * KSLICE)
+                if c + 1 < C:
+                    chunk_copy(c + 1, n).start()
+            for j, cols in slices(k):
                 hi, lo = split(dsn[rows, cols])
                 both[j % 2] += nt(mm[:, cols], hi)
                 small[j % 2] += nt(mm[0:Rp, cols], lo)
-            if k == NK // 2 - 1:
-                middle(c)
         for i in range(2):
             halves[i] = both[i][0:Rp] + (both[i][Rp:] + small[i])
-        if c == 0:
-            resp_copy.start()
-            path_copy.start()
-            index_copy.start()
-            pl.semaphore_wait(barrier, len(peers))
         for g, (q, fg, pg) in enumerate(groups):
             def join(n, carry, g=g, pg=pg):
                 at = pl.ds(pl.multiple_of(base[g] + n * pg, 8), pg)
@@ -226,33 +248,26 @@
             if g == 0 or (g == 1 and c < C - 1):
                 send(g, c)
 
-    def middle(c):
-        if c == min(2, C - 1):
-            resp_copy.wait()
-        if c >= 2:
-            total(0, c - 2)
-
-    for c in range(C):
+    with jax.named_scope("fit0"):
+        fit_head()
+    for c in range(HEAD, C):
         with jax.named_scope(f"fit{c}"):
-            fit(c, middle)
+            fit(c)
+    resp_copy.wait()
     end = C - 1
     with jax.named_scope("sum2"):
-        for c in range(max(C - 2, 0), end):
+        for c in range(end):
             total(0, c)
-    with jax.named_scope("early"):
-        for g in range(1, min(2, G)):
-            for c in range(max(C - 2, 0)):
-                total(g, c)
     with jax.named_scope("sum3"):
         total(0, end)
+    for c in range(C):
+        with jax.named_scope(f"keep{c}"):
+            keep(0, c)
     with jax.named_scope("early2"):
         for g in range(1, min(2, G)):
             send(g, end)
-            for c in range(max(C - 2, 0), end):
+            for c in range(end):
                 total(g, c)
-    for c in range(C):
-        with jax.named_scope(f"keep{c}"):
-            keep(0, c)
 
     def tile_at(t):
         return pl.ds(pl.multiple_of(t * TILE, TILE), TILE)
@@ -319,25 +334,23 @@
             forward(g, t)
 
     for g in range(G):
-        mark = 2 * T // 16
+        mark = (5 if g else 11) * T // 16
         with jax.named_scope(f"grad{g}_0"):
             sweep(g, rr[g], 0, mark)
         with jax.named_scope(f"round{g}"):
             if g + 1 < G:
-                if g == 0:
-                    total(1, end)
-                if g + 2 < G:
-                    for c in range(C):
-                        send(g + 2, c)
+                for c in range(C) if g else [end]:
+                    total(g + 1, c)
+            if g + 2 < G:
+                for c in range(C):
+                    send(g + 2, c)
         with jax.named_scope(f"grad{g}_1"):
             sweep(g, rr[g], mark, T)
             flush(g)
         with jax.named_scope(f"last{g}"):
-            for c in range(C):
-                if g + 1 < G:
+            if g + 1 < G:
+                for c in range(C):
                     keep(g + 1, c)
-                if g + 2 < G:
-                    total(g + 2, c)
 
     path_copy.wait()
     index_copy.wait()

time: 79.8 us -> 79.2 us (level)
  no operation moved by 1% of the time
where the time goes in v3:
time: 79.2 us; the launch traced here: 79 us
  Pallas kernels  76.7 us (97%)
  local copies, waits for them, and re-layouts  1.66 us (2%)
    pallas_call x1, Pallas kernels, body(): pl.pallas_call(functools.partial(kernel, cfg), out_shape=(pltpu.VMEM((rs,...  76.7 us

profile of v3, /device:TPU:0, one launch (start us, length us, event | category | flops | bytes accessed | tf_op | source)
XLA Modules:
  0.0 79.0 jit_solution(17472032102062835811)
XLA Ops:
  0.6 76.7 %shard_map.93 = (f32[48,8192]{1,0:T(8,128)S(1)}, f32[8,128]{1,0:T(8,128)S(1)}) custom-call(f32[1024,8192]{1,0:T(8,128)} %design.1, f32[2,2,48,8192]{3,2,1,0:T(8,128)} %bitcast.10, s32[4,48,8192]{2,1,0:T(8,128)} %bitcast.11, f32[192,1024]{1,0:T(8,128)} %response.1, f32[16,48]{1,0:T(8,128)} %bitcast.12, s32[1,48]{1,0:T(1,128)} %bitcast.13), custom_call_target="tpu_custom_call" | custom-call | tf_op jit(solution)/shard_map/pallas_call | solution.py:454
  77.3 0.5 slice_bitcast_fusion
  77.9 1.1 %copy.11 = f32[48,8192]{1,0:T(8,128)} copy(f32[48,8192]{1,0:T(8,128)S(1)} %get-tuple-element.11) | data formatting | bytes 3145728

commit v4 on v3

--- a/solution.py
+++ b/solution.py
@@ -334,7 +334,7 @@
             forward(g, t)
 
     for g in range(G):
-        mark = (5 if g else 11) * T // 16
+        mark = (9 if g else 11) * T // 16
         with jax.named_scope(f"grad{g}_0"):
             sweep(g, rr[g], 0, mark)
         with jax.named_scope(f"round{g}"):

time: 79.2 us -> 79.2 us (level)
  no operation moved by 1% of the time
where the time goes in v4:
time: 79.2 us; the launch traced here: 79.1 us
  Pallas kernels  76.8 us (97%)
  local copies, waits for them, and re-layouts  1.66 us (2%)
    pallas_call x1, Pallas kernels, body(): pl.pallas_call(functools.partial(kernel, cfg), out_shape=(pltpu.VMEM((rs,...  76.8 us

profile of v4, /device:TPU:0, one launch (start us, length us, event | category | flops | bytes accessed | tf_op | source)
XLA Modules:
  0.0 79.1 jit_solution(9839228686420720609)
XLA Ops:
  0.6 76.8 %shard_map.93 = (f32[48,8192]{1,0:T(8,128)S(1)}, f32[8,128]{1,0:T(8,128)S(1)}) custom-call(f32[1024,8192]{1,0:T(8,128)} %design.1, f32[2,2,48,8192]{3,2,1,0:T(8,128)} %bitcast.10, s32[4,48,8192]{2,1,0:T(8,128)} %bitcast.11, f32[192,1024]{1,0:T(8,128)} %response.1, f32[16,48]{1,0:T(8,128)} %bitcast.12, s32[1,48]{1,0:T(1,128)} %bitcast.13), custom_call_target="tpu_custom_call" | custom-call | tf_op jit(solution)/shard_map/pallas_call | solution.py:454
  77.4 0.5 slice_bitcast_fusion
  77.9 1.1 %copy.11 = f32[48,8192]{1,0:T(8,128)} copy(f32[48,8192]{1,0:T(8,128)S(1)} %get-tuple-element.11) | data formatting | bytes 3145728
